TPU v7x, 32 devices: a whole 2x2x4 slice. The times are simulated.
32 devices in a mesh: kx: 4 (over z), ky: 4 (over y, x), kz: 2 (over core).
Axes of the slice: x: 2, y: 2, z: 4, core: 2. Of those that a mesh axis runs over, the one named last changes fastest.
Arguments:
- u_start: float32 [4, 4, 8, 2, 128, 128], P('kx', 'ky', 'kz'), may hold values from -1 to 1, as said below
- intersections: float32 [4, 4, 8, 12, 2, 128, 128], P('kx', 'ky', 'kz'), may hold values from -1.2 to 1.2, as said below
Outputs:
- u_final: float32 [4, 4, 8, 2, 128, 128], P('kx', 'ky', 'kz')
- centres: float32 [3, 3, 128], replicated
- spreads: float32 [3, 128], replicated
Inputs may be any that keep to these rules, and one draw needn't show every extreme that they name: `u_start`: each U(k) is unitary up to float32 rounding and close to the identity: every diagonal entry of U(k) has magnitude 0.7 or more. `intersections`: every diagonal entry of every M(k,b) has magnitude 0.45 or more and a phase within 1.9 of zero.
All inputs are finite; a program needn't handle non-finite values.
Results may differ from a plain program's by a relative error of at most 0.0003.
Values sent between devices are 32-bit elements; how exact they have to be, the bound alone decides.
A program may use at most 128 MiB of HBM per device.

v0:
```python
import jax
import jax.numpy as jnp
from jax import lax
from jax.sharding import PartitionSpec as P

ITERS = 3
OFFSETS = (
    (1, 1, 0),
    (1, -1, 0),
    (-1, 1, 0),
    (-1, -1, 0),
    (1, 0, 1),
    (1, 0, -1),
    (-1, 0, 1),
    (-1, 0, -1),
    (0, 1, 1),
    (0, 1, -1),
    (0, -1, 1),
    (0, -1, -1),
)
WEIGHT = 0.125
STEP_SIZE = 0.35
PRECISE = lax.Precision.HIGHEST


def extended(cells, sides, width):
    for axis, dim in sides:
        count = lax.axis_size(axis)
        head = lax.slice_in_dim(cells, 0, width, axis=dim)
        tail = lax.slice_in_dim(cells, cells.shape[dim] - width, cells.shape[dim], axis=dim)
        cells = jnp.concatenate(
            [
                lax.ppermute(tail, axis, [(i, (i + 1) % count) for i in range(count)]),
                cells,
                lax.ppermute(head, axis, [((i + 1) % count, i) for i in range(count)]),
            ],
            axis=dim,
        )
    return cells


def matmul(left, right):
    return jnp.einsum("...ij,...jk->...ik", left, right, precision=PRECISE)


def adjoint_product(left, right):
    return jnp.einsum("...ji,...jk->...ik", left, right, precision=PRECISE)


def complex_product(left_real, left_imag, right_real, right_imag):
    return (
        matmul(left_real, right_real) - matmul(left_imag, right_imag),
        matmul(left_real, right_imag) + matmul(left_imag, right_real),
    )


def gather_neighbours(unitary):
    extent_x = unitary.shape[0]
    extent_y = unitary.shape[1]
    extent_z = unitary.shape[2]
    padded = extended(unitary, (("kx", 0), ("ky", 1), ("kz", 2)), 1)
    pieces = []
    for offset in OFFSETS:
        pieces.append(
            padded[
                1 + offset[0] : 1 + offset[0] + extent_x,
                1 + offset[1] : 1 + offset[1] + extent_y,
                1 + offset[2] : 1 + offset[2] + extent_z,
            ]
        )
    return jnp.stack(pieces, axis=3)


def body(u_start, intersections):
    count_x = u_start.shape[0]
    count_y = u_start.shape[1]
    count_z = u_start.shape[2]
    width = u_start.shape[-1]
    total_points = (
        count_x
        * count_y
        * count_z
        * lax.axis_size("kx")
        * lax.axis_size("ky")
        * lax.axis_size("kz")
    )
    offset_table = jnp.array(OFFSETS, jnp.float32)
    identity = jnp.eye(width, dtype=jnp.float32)
    intersection_real = intersections[:, :, :, :, 0]
    intersection_imag = intersections[:, :, :, :, 1]
    unitary = u_start
    centre_list = []
    spread_list = []
    for iteration in range(ITERS):
        local_real = unitary[:, :, :, None, 0]
        local_imag = unitary[:, :, :, None, 1]
        left_real = adjoint_product(local_real, intersection_real) + adjoint_product(
            local_imag, intersection_imag
        )
        left_imag = adjoint_product(local_real, intersection_imag) - adjoint_product(
            local_imag, intersection_real
        )
        nearby = gather_neighbours(unitary)
        turned_real, turned_imag = complex_product(
            left_real, left_imag, nearby[:, :, :, :, 0], nearby[:, :, :, :, 1]
        )
        diagonal_real = jnp.diagonal(turned_real, axis1=-2, axis2=-1)
        diagonal_imag = jnp.diagonal(turned_imag, axis1=-2, axis2=-1)
        phases = jnp.arctan2(diagonal_imag, diagonal_real)
        magnitude = diagonal_real * diagonal_real + diagonal_imag * diagonal_imag
        first_sums = WEIGHT * jnp.einsum("xyzbn,bc->cn", phases, offset_table, precision=PRECISE)
        second_sums = WEIGHT * jnp.sum(1.0 - magnitude + phases * phases, axis=(0, 1, 2, 3))
        product_real = (
            turned_real * diagonal_real[..., None, :] + turned_imag * diagonal_imag[..., None, :]
        )
        product_imag = (
            turned_imag * diagonal_real[..., None, :] - turned_real * diagonal_imag[..., None, :]
        )
        first_total, second_total = lax.psum((first_sums, second_sums), ("kx", "ky", "kz"))
        centres = -first_total / total_points
        spreads = second_total / total_points - jnp.sum(centres * centres, axis=0)
        centre_list.append(centres)
        spread_list.append(spreads)
        shifted = phases + jnp.einsum("bc,cn->bn", offset_table, centres, precision=PRECISE)
        scaled = (shifted / magnitude)[..., None, :]
        summed_real = jnp.sum(product_real - product_imag * scaled, axis=3)
        summed_imag = jnp.sum(product_imag + product_real * scaled, axis=3)
        gradient_real = 2.0 * WEIGHT * (summed_real - jnp.swapaxes(summed_real, -1, -2))
        gradient_imag = 2.0 * WEIGHT * (summed_imag + jnp.swapaxes(summed_imag, -1, -2))
        change_real = STEP_SIZE * gradient_real
        change_imag = STEP_SIZE * gradient_imag
        inner_real = 0.5 * identity + change_real / 6.0
        inner_imag = change_imag / 6.0
        middle_real, middle_imag = complex_product(change_real, change_imag, inner_real, inner_imag)
        middle_real = identity + middle_real
        exponent_real, exponent_imag = complex_product(
            change_real, change_imag, middle_real, middle_imag
        )
        exponent_real = identity + exponent_real
        update_real, update_imag = complex_product(
            unitary[:, :, :, 0], unitary[:, :, :, 1], exponent_real, exponent_imag
        )
        unitary = jnp.stack([update_real, update_imag], axis=3)
    return (unitary, jnp.stack(centre_list), jnp.stack(spread_list))


def solution(mesh):
    in_specs = (P("kx", "ky", "kz", None, None, None), P("kx", "ky", "kz", None, None, None, None))
    out_specs = (P("kx", "ky", "kz", None, None, None), P(), P())
    return jax.shard_map(body, mesh=mesh, in_specs=in_specs, out_specs=out_specs, check_vma=False)
```

profile of v0, /device:TPU:0, one launch (start us, length us, event | category | flops | bytes accessed | tf_op | source)
XLA Modules:
  0.0 661.2 jit_solution(17291030890249032201)
XLA Ops:
  1.8 3.1 collective-permute-start
  7.0 12.8 %collective-permute-done = f32[1,1,4,2,128,128]{5,4,2,3,1,0:T(8,128)S(1)} collective-permute-done((f32[1,1,4,2,128,128]{5,4,2,3,1,0:T(8,128)S(1)}, f32[1,1,4,2,128,128]{5,4,2,3,1,0:T(8,128)S(1)}, u32[]{:S(2)}, u32[]{:S(2)}) %collective-permute-start) | collective-permute-done | bytes 524320 | tf_op jit(solution)/shard_map/ppermute | solution.py:33
  20.9 8.7 %collective-permute-done.1 = f32[1,1,4,2,128,128]{5,4,2,3,1,0:T(8,128)S(1)} collective-permute-done((f32[1,1,4,2,128,128]{5,4,2,3,1,0:T(8,128)S(1)}, f32[1,1,4,2,128,128]{5,4,2,3,1,0:T(8,128)S(1)}, u32[]{:S(2)}, u32[]{:S(2)}) %collective-permute-start.1) | collective-permute-done | bytes 524320 | tf_op jit(solution)/shard_map/ppermute | solution.py:35
  32.5 7.0 %fusion.10 = f32[4,12,128,128]{3,2,1,0:T(8,128)S(1)} fusion(f32[1,1,4,12,2,128,128]{6,5,4,3,2,1,0:T(8,128)} %param.4, f32[1,1,4,2,128,128]{5,4,3,2,1,0:T(8,128)S(1)} %copy-done.1), kind=kOutput, calls=%fused_computation.22 | convolution fusion | flops 1207959552 | bytes 6553600 | tf_op jit(solution)/shard_map/...ji,...jk->...ik/dot_general | solution.py:47
  39.6 5.1 fusion.8
  44.7 5.2 fusion.94
  49.9 5.1 fusion.97
  55.0 12.8 %collective-permute-done.3 = f32[3,1,4,2,128,128]{5,4,2,3,1,0:T(8,128)S(1)} collective-permute-done((f32[3,1,4,2,128,128]{5,4,2,3,1,0:T(8,128)S(1)}, f32[3,1,4,2,128,128]{5,4,2,3,1,0:T(8,128)S(1)}, u32[]{:S(2)}, u32[]{:S(2)}) %collective-permute-start.3) | collective-permute-done | bytes 1572896 | tf_op jit(solution)/shard_map/ppermute | solution.py:33
  67.8 32.2 %collective-permute-done.2 = f32[3,1,4,2,128,128]{5,4,2,3,1,0:T(8,128)S(1)} collective-permute-done((f32[3,1,4,2,128,128]{5,4,2,3,1,0:T(8,128)S(1)}, f32[3,1,4,2,128,128]{5,4,2,3,1,0:T(8,128)S(1)}, u32[]{:S(2)}, u32[]{:S(2)}) %collective-permute-start.2) | collective-permute-done | bytes 1572896 | tf_op jit(solution)/shard_map/ppermute | solution.py:35
  105.2 5.7 fusion.40
  110.9 5.5 fusion.42
  116.3 6.0 fusion.71
  122.4 7.2 %fusion.68 = f32[4,12,128,128]{3,2,1,0:T(8,128)} fusion(f32[4,12,128,128]{3,2,1,0:T(8,128)S(1)} %fusion.42, f32[1,1,4,12,2,128,128]{6,5,3,2,4,1,0:T(8,128)S(1)} %fusion.152, f32[4,12,128,128]{3,2,1,0:T(8,128)S(1)} %fusion.94), kind=kOutput, calls=%fused_computation.92 | convolution fusion | flops 1208745984 | bytes 12582912 | tf_op jit(solution)/shard_map/...ij,...jk->...ik/dot_general | solution.py:43
  129.6 18.5 %copy.238 = f32[4,12,128,128]{1,0,3,2:T(4,128)} copy(f32[4,12,128,128]{3,2,1,0:T(8,128)} %fusion.68) | data formatting | bytes 6291456 | tf_op jit(solution)/shard_map/sub | solution.py:52
  151.4 16.8 %copy.243 = f32[4,12,128,128]{1,0,3,2:T(4,128)} copy(f32[4,12,128,128]{3,2,1,0:T(8,128)S(1)} %fusion.71) | data formatting | bytes 6291456 | tf_op jit(solution)/shard_map/add | solution.py:53
  173.0 39.8 %psum.42 = f32[3,128]{1,0:T(4,128)S(1)} all-reduce(f32[3,128]{1,0:T(4,128)} %fusion.122), channel_id=1, replica_groups=mesh['kx'=4,'ky'=4,'kz'=2] {'kx','ky','kz'}, use_global_device_ids=true, to_apply=%region_1.2 | all-reduce | flops 384 | bytes 3072 | tf_op jit(solution)/shard_map/psum | solution.py:119
  215.0 4.2 add_reduce_fusion.2
  228.6 12.7 %collective-permute-done.7 = f32[1,1,4,2,128,128]{4,5,2,3,1,0:T(8,128)S(1)} collective-permute-done((f32[1,1,4,2,128,128]{4,5,2,3,1,0:T(8,128)S(1)}, f32[1,1,4,2,128,128]{4,5,2,3,1,0:T(8,128)S(1)}, u32[]{:S(2)}, u32[]{:S(2)}) %collective-permute-start.7) | collective-permute-done | bytes 524320 | tf_op jit(solution)/shard_map/ppermute | solution.py:35
  241.3 9.3 %collective-permute-done.6 = f32[1,1,4,2,128,128]{4,5,2,3,1,0:T(8,128)S(1)} collective-permute-done((f32[1,1,4,2,128,128]{4,5,2,3,1,0:T(8,128)S(1)}, f32[1,1,4,2,128,128]{4,5,2,3,1,0:T(8,128)S(1)}, u32[]{:S(2)}, u32[]{:S(2)}) %collective-permute-start.6) | collective-permute-done | bytes 524320 | tf_op jit(solution)/shard_map/ppermute | solution.py:33
  257.0 3.0 fusion.4
  260.0 3.0 fusion.100
  263.1 26.0 %collective-permute-done.9 = f32[3,1,4,2,128,128]{4,5,2,3,1,0:T(8,128)S(1)} collective-permute-done((f32[3,1,4,2,128,128]{4,5,2,3,1,0:T(8,128)S(1)}, f32[3,1,4,2,128,128]{4,5,2,3,1,0:T(8,128)S(1)}, u32[]{:S(2)}, u32[]{:S(2)}) %collective-permute-start.9) | collective-permute-done | bytes 1572896 | tf_op jit(solution)/shard_map/ppermute | solution.py:33
  289.1 31.8 %collective-permute-done.8 = f32[3,1,4,2,128,128]{4,5,2,3,1,0:T(8,128)S(1)} collective-permute-done((f32[3,1,4,2,128,128]{4,5,2,3,1,0:T(8,128)S(1)}, f32[3,1,4,2,128,128]{4,5,2,3,1,0:T(8,128)S(1)}, u32[]{:S(2)}, u32[]{:S(2)}) %collective-permute-start.8) | collective-permute-done | bytes 1572896 | tf_op jit(solution)/shard_map/ppermute | solution.py:35
  321.6 3.0 fusion.103
  327.2 6.8 %fusion.34 = f32[4,12,128,128]{3,2,1,0:T(8,128)S(1)} fusion(f32[4,128,12,128]{3,1,2,0:T(8,128)S(1)} %fusion.103, f32[4,12,128,128]{2,3,0,1:T(8,128)S(1)} %get-tuple-element.33), kind=kOutput, calls=%fused_computation.46 | convolution fusion | flops 1207959552 | bytes 9437184 | tf_op jit(solution)/shard_map/...ij,...jk->...ik/dot_general | solution.py:43
  334.0 6.7 %fusion.32 = f32[4,12,128,128]{3,2,1,0:T(8,128)S(1)} fusion(f32[4,128,12,128]{3,1,2,0:T(8,128)S(1)} %fusion.103, f32[4,12,128,128]{2,3,0,1:T(8,128)S(1)} %get-tuple-element.34), kind=kOutput, calls=%fused_computation.44 | convolution fusion | flops 1207959552 | bytes 9437184 | tf_op jit(solution)/shard_map/...ij,...jk->...ik/dot_general | solution.py:43
  340.7 8.6 %fusion.74 = f32[4,12,128,128]{3,2,1,0:T(8,128)} fusion(f32[4,12,128,128]{3,2,1,0:T(8,128)S(1)} %fusion.34, f32[4,12,128,128]{2,3,0,1:T(8,128)S(1)} %get-tuple-element.34, f32[4,128,12,128]{3,1,2,0:T(8,128)S(1)} %fusion.100), kind=kOutput, calls=%fused_computation.94 | convolution fusion | flops 1208745984 | bytes 12582912 | tf_op jit(solution)/shard_map/...ij,...jk->...ik/dot_general | solution.py:43
  349.3 8.4 %fusion.79 = f32[4,12,128,128]{3,2,1,0:T(8,128)} fusion(f32[4,12,128,128]{3,2,1,0:T(8,128)S(1)} %fusion.32, f32[4,12,128,128]{2,3,0,1:T(8,128)S(1)} %get-tuple-element.33, f32[4,128,12,128]{3,1,2,0:T(8,128)S(1)} %fusion.100), kind=kOutput, calls=%fused_computation.95 | convolution fusion | flops 1208745984 | bytes 12582912 | tf_op jit(solution)/shard_map/...ij,...jk->...ik/dot_general | solution.py:43
  357.6 18.5 %copy.266 = f32[4,12,128,128]{1,0,3,2:T(4,128)} copy(f32[4,12,128,128]{3,2,1,0:T(8,128)} %fusion.79) | data formatting | bytes 6291456 | tf_op jit(solution)/shard_map/add | solution.py:53
  378.3 18.5 %copy.261 = f32[4,12,128,128]{1,0,3,2:T(4,128)} copy(f32[4,12,128,128]{3,2,1,0:T(8,128)} %fusion.74) | data formatting | bytes 6291456 | tf_op jit(solution)/shard_map/sub | solution.py:52
  399.2 39.5 %psum.43 = f32[3,128]{1,0:T(4,128)S(1)} all-reduce(f32[3,128]{1,0:T(4,128)S(1)} %fusion.121), channel_id=1, replica_groups=mesh['kx'=4,'ky'=4,'kz'=2] {'kx','ky','kz'}, use_global_device_ids=true, to_apply=%region_5.6 | all-reduce | flops 384 | bytes 3072 | tf_op jit(solution)/shard_map/psum | solution.py:119
  439.0 4.4 add_reduce_fusion.1
  452.2 12.3 %collective-permute-done.13 = f32[1,1,4,2,128,128]{5,4,2,3,1,0:T(8,128)S(1)} collective-permute-done((f32[1,1,4,2,128,128]{5,4,2,3,1,0:T(8,128)S(1)}, f32[1,1,4,2,128,128]{5,4,2,3,1,0:T(8,128)S(1)}, u32[]{:S(2)}, u32[]{:S(2)}) %collective-permute-start.13) | collective-permute-done | bytes 524320 | tf_op jit(solution)/shard_map/ppermute | solution.py:35
  464.5 10.0 %collective-permute-done.12 = f32[1,1,4,2,128,128]{5,4,2,3,1,0:T(8,128)S(1)} collective-permute-done((f32[1,1,4,2,128,128]{5,4,2,3,1,0:T(8,128)S(1)}, f32[1,1,4,2,128,128]{5,4,2,3,1,0:T(8,128)S(1)}, u32[]{:S(2)}, u32[]{:S(2)}) %collective-permute-start.12) | collective-permute-done | bytes 524320 | tf_op jit(solution)/shard_map/ppermute | solution.py:33
  478.1 3.0 fusion
  481.1 3.0 fusion.2
  484.1 3.1 fusion.109
  487.2 3.1 fusion.106
  490.3 22.6 %collective-permute-done.15 = f32[3,1,4,2,128,128]{5,4,2,3,1,0:T(8,128)S(1)} collective-permute-done((f32[3,1,4,2,128,128]{5,4,2,3,1,0:T(8,128)S(1)}, f32[3,1,4,2,128,128]{5,4,2,3,1,0:T(8,128)S(1)}, u32[]{:S(2)}, u32[]{:S(2)}) %collective-permute-start.15) | collective-permute-done | bytes 1572896 | tf_op jit(solution)/shard_map/ppermute | solution.py:33
  512.9 30.0 %collective-permute-done.14 = f32[3,1,4,2,128,128]{5,4,2,3,1,0:T(8,128)S(1)} collective-permute-done((f32[3,1,4,2,128,128]{5,4,2,3,1,0:T(8,128)S(1)}, f32[3,1,4,2,128,128]{5,4,2,3,1,0:T(8,128)S(1)}, u32[]{:S(2)}, u32[]{:S(2)}) %collective-permute-start.14) | collective-permute-done | bytes 1572896 | tf_op jit(solution)/shard_map/ppermute | solution.py:35
  548.9 3.9 fusion.26
  552.8 3.5 fusion.24
  556.3 5.3 fusion.84
  561.6 5.3 fusion.89
  566.9 18.5 %copy.294 = f32[4,12,128,128]{1,0,3,2:T(4,128)} copy(f32[4,12,128,128]{3,2,1,0:T(8,128)} %fusion.89) | data formatting | bytes 6291456 | tf_op jit(solution)/shard_map/add | solution.py:53
  587.4 18.5 %copy.289 = f32[4,12,128,128]{1,0,3,2:T(4,128)} copy(f32[4,12,128,128]{3,2,1,0:T(8,128)} %fusion.84) | data formatting | bytes 6291456 | tf_op jit(solution)/shard_map/sub | solution.py:52
  608.3 39.9 %all-reduce = (f32[3,128]{1,0:T(4,128)S(1)}, f32[128]{0:T(128)S(1)}, f32[128]{0:T(128)S(1)}, f32[128]{0:T(128)S(1)}) all-reduce(f32[3,128]{1,0:T(4,128)S(1)} %fusion.120, f32[128]{0:T(128)S(1)} %broadcast_multiply_fusion, f32[128]{0:T(128)S(1)} %broadcast_multiply_fusion.1, ...), channel_id=1, replica_groups=mesh['kx'=4,'ky'=4,'kz'=2] {'kx','ky','kz'}, use_global_device_ids=true, to_apply=%region_9.10 | all-reduce | flops 768 | bytes 6144 | tf_op jit(solution)/shard_map/psum | solution.py:119
  648.7 4.5 subtract_reduce_fusion
  (194 shorter events, 76.7 us)
Async XLA Ops:
  0.6 31.9 %copy-start.1 = (f32[1,1,4,2,128,128]{5,4,3,2,1,0:T(8,128)S(1)}, f32[1,1,4,2,128,128]{5,4,3,2,1,0:T(8,128)}, u32[]{:S(2)}) copy-start(f32[1,1,4,2,128,128]{5,4,3,2,1,0:T(8,128)} %param.3) | copy-start | bytes 1572868
  1.8 17.9 %collective-permute-start = (f32[1,1,4,2,128,128]{5,4,2,3,1,0:T(8,128)S(1)}, f32[1,1,4,2,128,128]{5,4,2,3,1,0:T(8,128)S(1)}, u32[]{:S(2)}, u32[]{:S(2)}) collective-permute-start(f32[1,1,4,2,128,128]{5,4,2,3,1,0:T(8,128)S(1)} %copy.219), channel_id=1, source_target_pairs={{0,8},{8,16},{16,24},{24,0},{1,9},{9,17},{17,25},{25,1},{2,10},{10... | collective-permute-start | bytes 1572872 | tf_op jit(solution)/shard_map/ppermute | solution.py:33
  4.9 24.6 %collective-permute-start.1 = (f32[1,1,4,2,128,128]{5,4,2,3,1,0:T(8,128)S(1)}, f32[1,1,4,2,128,128]{5,4,2,3,1,0:T(8,128)S(1)}, u32[]{:S(2)}, u32[]{:S(2)}) collective-permute-start(f32[1,1,4,2,128,128]{5,4,2,3,1,0:T(8,128)S(1)} %copy.219), channel_id=1, source_target_pairs={{8,0},{16,8},{24,16},{0,24},{9,1},{17,9},{25,17},{1,25},{10,2},{18... | collective-permute-start | bytes 1572872 | tf_op jit(solution)/shard_map/ppermute | solution.py:35
  29.6 10.1 %copy-start = (f32[1,1,4,12,2,128,128]{6,5,4,3,2,1,0:T(8,128)S(1)}, f32[1,1,4,12,2,128,128]{6,5,4,3,2,1,0:T(8,128)}, u32[]{:S(2)}) copy-start(f32[1,1,4,12,2,128,128]{6,5,4,3,2,1,0:T(8,128)} %param.4) | copy-start | bytes 18874372
  29.6 38.2 %collective-permute-start.3 = (f32[3,1,4,2,128,128]{5,4,2,3,1,0:T(8,128)S(1)}, f32[3,1,4,2,128,128]{5,4,2,3,1,0:T(8,128)S(1)}, u32[]{:S(2)}, u32[]{:S(2)}) collective-permute-start(f32[3,1,4,2,128,128]{5,4,2,3,1,0:T(8,128)S(1)} %constant_dynamic-update-slice_fusion), channel_id=1, source_target_pairs={{0,2},{2,4},{4,6},{6,0},{1,3},{3,5},{5,7},{7,1},{8,10},{10,12},{12... | collective-permute-start | bytes 4718600 | tf_op jit(solution)/shard_map/ppermute | solution.py:33
  31.1 68.9 %collective-permute-start.2 = (f32[3,1,4,2,128,128]{5,4,2,3,1,0:T(8,128)S(1)}, f32[3,1,4,2,128,128]{5,4,2,3,1,0:T(8,128)S(1)}, u32[]{:S(2)}, u32[]{:S(2)}) collective-permute-start(f32[3,1,4,2,128,128]{5,4,2,3,1,0:T(8,128)S(1)} %constant_dynamic-update-slice_fusion), channel_id=1, source_target_pairs={{2,0},{4,2},{6,4},{0,6},{3,1},{5,3},{7,5},{1,7},{10,8},{12,10},{14... | collective-permute-start | bytes 4718600 | tf_op jit(solution)/shard_map/ppermute | solution.py:35
  100.3 2.9 collective-permute-start.4
  100.4 4.5 collective-permute-start.5
  151.4 20.8 %copy-start.3 = (f32[12,3]{1,0:T(8,128)S(1)}, f32[12,3]{1,0:T(8,128)}, u32[]{:S(2)}) copy-start(f32[12,3]{1,0:T(8,128)} %constant.59.clone) | copy-start | bytes 436
  221.1 32.9 %slice-start = ((s8[6291456]{0:T(1024)(128)(4,1)}), s8[4194304]{0:T(1024)(128)(4,1)S(1)}, s32[]{:S(2)}) async-start(s8[6291456]{0:T(1024)(128)(4,1)} %bitcast.643), calls=%async_computation | async-start | bytes 8388608
  221.5 2.5 copy-start.2
  224.0 30.0 %slice-start.1 = ((s8[6291456]{0:T(1024)(128)(4,1)}), s8[2097152]{0:T(1024)(128)(4,1)S(1)}, s32[]{:S(2)}) async-start(s8[6291456]{0:T(1024)(128)(4,1)} %bitcast.643), calls=%async_computation.1 | async-start | bytes 4194304
  226.5 14.8 %collective-permute-start.7 = (f32[1,1,4,2,128,128]{4,5,2,3,1,0:T(8,128)S(1)}, f32[1,1,4,2,128,128]{4,5,2,3,1,0:T(8,128)S(1)}, u32[]{:S(2)}, u32[]{:S(2)}) collective-permute-start(f32[1,1,4,2,128,128]{4,5,2,3,1,0:T(8,128)S(1)} %pad_maximum_fusion.47), channel_id=1, source_target_pairs={{8,0},{16,8},{24,16},{0,24},{9,1},{17,9},{25,17},{1,25},{10,2},{18... | collective-permute-start | bytes 1572872 | tf_op jit(solution)/shard_map/ppermute | solution.py:35
  228.1 22.6 %collective-permute-start.6 = (f32[1,1,4,2,128,128]{4,5,2,3,1,0:T(8,128)S(1)}, f32[1,1,4,2,128,128]{4,5,2,3,1,0:T(8,128)S(1)}, u32[]{:S(2)}, u32[]{:S(2)}) collective-permute-start(f32[1,1,4,2,128,128]{4,5,2,3,1,0:T(8,128)S(1)} %pad_maximum_fusion.47), channel_id=1, source_target_pairs={{0,8},{8,16},{16,24},{24,0},{1,9},{9,17},{17,25},{25,1},{2,10},{10... | collective-permute-start | bytes 1572872 | tf_op jit(solution)/shard_map/ppermute | solution.py:33
  250.8 38.2 %collective-permute-start.9 = (f32[3,1,4,2,128,128]{4,5,2,3,1,0:T(8,128)S(1)}, f32[3,1,4,2,128,128]{4,5,2,3,1,0:T(8,128)S(1)}, u32[]{:S(2)}, u32[]{:S(2)}) collective-permute-start(f32[3,1,4,2,128,128]{4,5,2,3,1,0:T(8,128)S(1)} %pad_maximum_fusion), channel_id=1, source_target_pairs={{0,2},{2,4},{4,6},{6,0},{1,3},{3,5},{5,7},{7,1},{8,10},{10,12},{12... | collective-permute-start | bytes 4718600 | tf_op jit(solution)/shard_map/ppermute | solution.py:33
  253.2 67.6 %collective-permute-start.8 = (f32[3,1,4,2,128,128]{4,5,2,3,1,0:T(8,128)S(1)}, f32[3,1,4,2,128,128]{4,5,2,3,1,0:T(8,128)S(1)}, u32[]{:S(2)}, u32[]{:S(2)}) collective-permute-start(f32[3,1,4,2,128,128]{4,5,2,3,1,0:T(8,128)S(1)} %pad_maximum_fusion), channel_id=1, source_target_pairs={{2,0},{4,2},{6,4},{0,6},{3,1},{5,3},{7,5},{1,7},{10,8},{12,10},{14... | collective-permute-start | bytes 4718600 | tf_op jit(solution)/shard_map/ppermute | solution.py:35
  321.1 4.6 collective-permute-start.11
  321.1 4.5 collective-permute-start.10
  444.5 33.6 %slice-start.2 = ((s8[6291456]{0:T(1024)(128)(4,1)}), s8[4194304]{0:T(1024)(128)(4,1)S(1)}, s32[]{:S(2)}) async-start(s8[6291456]{0:T(1024)(128)(4,1)} %bitcast.645), calls=%async_computation.2 | async-start | bytes 8388608
  447.0 5.2 copy-start.4
  447.4 30.6 %slice-start.3 = ((s8[6291456]{0:T(1024)(128)(4,1)}), s8[2097152]{0:T(1024)(128)(4,1)S(1)}, s32[]{:S(2)}) async-start(s8[6291456]{0:T(1024)(128)(4,1)} %bitcast.645), calls=%async_computation.3 | async-start | bytes 4194304
  449.9 14.6 %collective-permute-start.13 = (f32[1,1,4,2,128,128]{5,4,2,3,1,0:T(8,128)S(1)}, f32[1,1,4,2,128,128]{5,4,2,3,1,0:T(8,128)S(1)}, u32[]{:S(2)}, u32[]{:S(2)}) collective-permute-start(f32[1,1,4,2,128,128]{5,4,2,3,1,0:T(8,128)S(1)} %pad_maximum_fusion.48), channel_id=1, source_target_pairs={{8,0},{16,8},{24,16},{0,24},{9,1},{17,9},{25,17},{1,25},{10,2},{18... | collective-permute-start | bytes 1572872 | tf_op jit(solution)/shard_map/ppermute | solution.py:35
  452.2 22.4 %collective-permute-start.12 = (f32[1,1,4,2,128,128]{5,4,2,3,1,0:T(8,128)S(1)}, f32[1,1,4,2,128,128]{5,4,2,3,1,0:T(8,128)S(1)}, u32[]{:S(2)}, u32[]{:S(2)}) collective-permute-start(f32[1,1,4,2,128,128]{5,4,2,3,1,0:T(8,128)S(1)} %pad_maximum_fusion.48), channel_id=1, source_target_pairs={{0,8},{8,16},{16,24},{24,0},{1,9},{9,17},{17,25},{25,1},{2,10},{10... | collective-permute-start | bytes 1572872 | tf_op jit(solution)/shard_map/ppermute | solution.py:33
  474.7 38.2 %collective-permute-start.15 = (f32[3,1,4,2,128,128]{5,4,2,3,1,0:T(8,128)S(1)}, f32[3,1,4,2,128,128]{5,4,2,3,1,0:T(8,128)S(1)}, u32[]{:S(2)}, u32[]{:S(2)}) collective-permute-start(f32[3,1,4,2,128,128]{5,4,2,3,1,0:T(8,128)S(1)} %pad_maximum_fusion.1), channel_id=1, source_target_pairs={{0,2},{2,4},{4,6},{6,0},{1,3},{3,5},{5,7},{7,1},{8,10},{10,12},{12... | collective-permute-start | bytes 4718600 | tf_op jit(solution)/shard_map/ppermute | solution.py:33
  476.1 66.8 %collective-permute-start.14 = (f32[3,1,4,2,128,128]{5,4,2,3,1,0:T(8,128)S(1)}, f32[3,1,4,2,128,128]{5,4,2,3,1,0:T(8,128)S(1)}, u32[]{:S(2)}, u32[]{:S(2)}) collective-permute-start(f32[3,1,4,2,128,128]{5,4,2,3,1,0:T(8,128)S(1)} %pad_maximum_fusion.1), channel_id=1, source_target_pairs={{2,0},{4,2},{6,4},{0,6},{3,1},{5,3},{7,5},{1,7},{10,8},{12,10},{14... | collective-permute-start | bytes 4718600 | tf_op jit(solution)/shard_map/ppermute | solution.py:35
  543.2 2.9 collective-permute-start.16
  543.3 4.5 collective-permute-start.17
where the time goes:
time: 672 us; the launch traced here: 661 us
  waiting for transfers between devices  229 us (34%)
  matrix products  137 us (20%)
  local copies, waits for them, and re-layouts  133 us (20%)
  blocking collectives  119 us (18%)
  starting transfers between devices  20.8 us (3%)
  other arithmetic  19.8 us (3%)
    ppermute x9, waiting for transfers between devices, extended(): lax.ppermute(head, axis, [((i + 1) % count, i) for i in range(count)])  133 us
    psum x3, blocking collectives, body(): lax.psum((first_sums, second_sums), ('kx', 'ky', 'kz'))  119 us
    ppermute x9, waiting for transfers between devices, extended(): lax.ppermute(tail, axis, [(i, (i + 1) % count) for i in range(count)])  96.8 us
    dot_general x48, matrix products, matmul(): return jnp.einsum('...ij,...jk->...ik', left, right, precision=PRECISE)  89 us
    sub x3, local copies, waits for them, and re-layouts, complex_product(): matmul(left_real, right_real) - matmul(left_imag, right_imag)  55.6 us
    add x3, local copies, waits for them, and re-layouts, complex_product(): matmul(left_real, right_imag) + matmul(left_imag, right_real)  53.8 us
    dot_general x12, matrix products, adjoint_product(): return jnp.einsum('...ji,...jk->...ik', left, right, precision=PRECISE)  46.7 us
  transfers between devices with their start and end apart: 18, of which 17 were waited for; matrix products, arithmetic and copies ran while one was open for 7% of the time, Pallas kernels for 0%

commit v1 on v0

--- a/solution.py
+++ b/solution.py
@@ -116,7 +116,9 @@
         product_imag = (
             turned_imag * diagonal_real[..., None, :] - turned_real * diagonal_imag[..., None, :]
         )
-        first_total, second_total = lax.psum((first_sums, second_sums), ("kx", "ky", "kz"))
+        first_total, second_total = lax.psum(
+            lax.psum((first_sums, second_sums), ("ky", "kz")), "kx"
+        )
         centres = -first_total / total_points
         spreads = second_total / total_points - jnp.sum(centres * centres, axis=0)
         centre_list.append(centres)

time: 672 us -> 618 us (0.920)
  blocking collectives: 119 us -> 75.1 us
  waiting for transfers between devices: 229 us -> 219 us
    psum x3 -> x6, blocking collectives: 119 us -> 75.1 us  [the longest x3 41.1 us: body(): lax.psum((first_sums, second_sums), ('ky', 'kz'))]
    ppermute x9, waiting for transfers between devices: 96.8 us -> 77.4 us  [extended(): lax.ppermute(tail, axis, [(i, (i + 1) % count) for i in range(count)])]
    ppermute x9, waiting for transfers between devices: 133 us -> 142 us  [extended(): lax.ppermute(head, axis, [((i + 1) % count, i) for i in range(count)])]
  transfers between devices with their start and end apart: 18 -> 18, of which waited for: 17 -> 15; matrix products, arithmetic and copies ran while one was open for 7% -> 8% of each run, Pallas kernels for 0% -> 0%
where the time goes in v1:
time: 618 us; the launch traced here: 606 us
  waiting for transfers between devices  219 us (35%)
  matrix products  137 us (22%)
  local copies, waits for them, and re-layouts  133 us (22%)
  blocking collectives  75.1 us (12%)
  starting transfers between devices  20.6 us (3%)
  other arithmetic  19.8 us (3%)
    ppermute x9, waiting for transfers between devices, extended(): lax.ppermute(head, axis, [((i + 1) % count, i) for i in range(count)])  142 us
    dot_general x48, matrix products, matmul(): return jnp.einsum('...ij,...jk->...ik', left, right, precision=PRECISE)  89 us
    ppermute x9, waiting for transfers between devices, extended(): lax.ppermute(tail, axis, [(i, (i + 1) % count) for i in range(count)])  77.4 us
    sub x3, local copies, waits for them, and re-layouts, complex_product(): matmul(left_real, right_real) - matmul(left_imag, right_imag)  55.6 us
    add x3, local copies, waits for them, and re-layouts, complex_product(): matmul(left_real, right_imag) + matmul(left_imag, right_real)  53.8 us
    dot_general x12, matrix products, adjoint_product(): return jnp.einsum('...ji,...jk->...ik', left, right, precision=PRECISE)  46.7 us
    psum x3, blocking collectives, body(): lax.psum((first_sums, second_sums), ('ky', 'kz'))  41.1 us
    psum x3, blocking collectives, body(): lax.psum(lax.psum((first_sums, second_sums), ('ky', 'kz')), 'kx')  34 us
  transfers between devices with their start and end apart: 18, of which 15 were waited for; matrix products, arithmetic and copies ran while one was open for 8% of the time, Pallas kernels for 0%

profile of v1, /device:TPU:0, one launch (start us, length us, event | category | flops | bytes accessed | tf_op | source)
XLA Modules:
  0.0 606.3 jit_solution(16136173356670745127)
XLA Ops:
  1.8 3.1 collective-permute-start
  7.0 12.8 %collective-permute-done = f32[1,1,4,2,128,128]{5,4,2,3,1,0:T(8,128)S(1)} collective-permute-done((f32[1,1,4,2,128,128]{5,4,2,3,1,0:T(8,128)S(1)}, f32[1,1,4,2,128,128]{5,4,2,3,1,0:T(8,128)S(1)}, u32[]{:S(2)}, u32[]{:S(2)}) %collective-permute-start) | collective-permute-done | bytes 524320 | tf_op jit(solution)/shard_map/ppermute | solution.py:33
  20.9 8.7 %collective-permute-done.1 = f32[1,1,4,2,128,128]{5,4,2,3,1,0:T(8,128)S(1)} collective-permute-done((f32[1,1,4,2,128,128]{5,4,2,3,1,0:T(8,128)S(1)}, f32[1,1,4,2,128,128]{5,4,2,3,1,0:T(8,128)S(1)}, u32[]{:S(2)}, u32[]{:S(2)}) %collective-permute-start.1) | collective-permute-done | bytes 524320 | tf_op jit(solution)/shard_map/ppermute | solution.py:35
  32.5 7.0 %fusion.10 = f32[4,12,128,128]{3,2,1,0:T(8,128)S(1)} fusion(f32[1,1,4,12,2,128,128]{6,5,4,3,2,1,0:T(8,128)} %param.4, f32[1,1,4,2,128,128]{5,4,3,2,1,0:T(8,128)S(1)} %copy-done.1), kind=kOutput, calls=%fused_computation.22 | convolution fusion | flops 1207959552 | bytes 6553600 | tf_op jit(solution)/shard_map/...ji,...jk->...ik/dot_general | solution.py:47
  39.6 5.1 fusion.8
  44.7 5.2 fusion.94
  49.9 5.1 fusion.97
  55.0 12.8 %collective-permute-done.3 = f32[3,1,4,2,128,128]{5,4,2,3,1,0:T(8,128)S(1)} collective-permute-done((f32[3,1,4,2,128,128]{5,4,2,3,1,0:T(8,128)S(1)}, f32[3,1,4,2,128,128]{5,4,2,3,1,0:T(8,128)S(1)}, u32[]{:S(2)}, u32[]{:S(2)}) %collective-permute-start.3) | collective-permute-done | bytes 1572896 | tf_op jit(solution)/shard_map/ppermute | solution.py:33
  67.8 32.2 %collective-permute-done.2 = f32[3,1,4,2,128,128]{5,4,2,3,1,0:T(8,128)S(1)} collective-permute-done((f32[3,1,4,2,128,128]{5,4,2,3,1,0:T(8,128)S(1)}, f32[3,1,4,2,128,128]{5,4,2,3,1,0:T(8,128)S(1)}, u32[]{:S(2)}, u32[]{:S(2)}) %collective-permute-start.2) | collective-permute-done | bytes 1572896 | tf_op jit(solution)/shard_map/ppermute | solution.py:35
  105.2 5.7 fusion.40
  110.9 5.5 fusion.42
  116.3 6.0 fusion.71
  122.4 7.2 %fusion.68 = f32[4,12,128,128]{3,2,1,0:T(8,128)} fusion(f32[4,12,128,128]{3,2,1,0:T(8,128)S(1)} %fusion.42, f32[1,1,4,12,2,128,128]{6,5,3,2,4,1,0:T(8,128)S(1)} %fusion.152, f32[4,12,128,128]{3,2,1,0:T(8,128)S(1)} %fusion.94), kind=kOutput, calls=%fused_computation.92 | convolution fusion | flops 1208745984 | bytes 12582912 | tf_op jit(solution)/shard_map/...ij,...jk->...ik/dot_general | solution.py:43
  129.6 18.5 %copy.238 = f32[4,12,128,128]{1,0,3,2:T(4,128)} copy(f32[4,12,128,128]{3,2,1,0:T(8,128)} %fusion.68) | data formatting | bytes 6291456 | tf_op jit(solution)/shard_map/sub | solution.py:52
  151.4 16.8 %copy.243 = f32[4,12,128,128]{1,0,3,2:T(4,128)} copy(f32[4,12,128,128]{3,2,1,0:T(8,128)S(1)} %fusion.71) | data formatting | bytes 6291456 | tf_op jit(solution)/shard_map/add | solution.py:53
  172.4 13.5 %psum.84 = f32[3,128]{1,0:T(4,128)} all-reduce(f32[3,128]{1,0:T(4,128)S(1)} %fusion.122), channel_id=1, replica_groups=mesh['kx'=4,'ky'=4,'kz'=2] {'ky','kz'}, use_global_device_ids=true, to_apply=%region_1.2 | all-reduce | flops 384 | bytes 3072 | tf_op jit(solution)/shard_map/psum | solution.py:120
  185.9 10.3 %psum.85 = f32[3,128]{1,0:T(4,128)S(1)} all-reduce(f32[3,128]{1,0:T(4,128)} %psum.84), channel_id=1, replica_groups=mesh['kx'=4,'ky'=4,'kz'=2] {'kx'}, use_global_device_ids=true, to_apply=%region_2.3 | all-reduce | flops 384 | bytes 3072 | tf_op jit(solution)/shard_map/psum | solution.py:119
  198.5 4.2 add_reduce_fusion.2
  212.1 19.8 %collective-permute-done.7 = f32[1,1,4,2,128,128]{4,5,2,3,1,0:T(8,128)S(1)} collective-permute-done((f32[1,1,4,2,128,128]{4,5,2,3,1,0:T(8,128)S(1)}, f32[1,1,4,2,128,128]{4,5,2,3,1,0:T(8,128)S(1)}, u32[]{:S(2)}, u32[]{:S(2)}) %collective-permute-start.7) | collective-permute-done | bytes 524320 | tf_op jit(solution)/shard_map/ppermute | solution.py:35
  241.3 3.0 fusion.100
  244.3 26.0 %collective-permute-done.9 = f32[3,1,4,2,128,128]{4,5,2,3,1,0:T(8,128)S(1)} collective-permute-done((f32[3,1,4,2,128,128]{4,5,2,3,1,0:T(8,128)S(1)}, f32[3,1,4,2,128,128]{4,5,2,3,1,0:T(8,128)S(1)}, u32[]{:S(2)}, u32[]{:S(2)}) %collective-permute-start.9) | collective-permute-done | bytes 1572896 | tf_op jit(solution)/shard_map/ppermute | solution.py:33
  270.3 29.0 %collective-permute-done.8 = f32[3,1,4,2,128,128]{4,5,2,3,1,0:T(8,128)S(1)} collective-permute-done((f32[3,1,4,2,128,128]{4,5,2,3,1,0:T(8,128)S(1)}, f32[3,1,4,2,128,128]{4,5,2,3,1,0:T(8,128)S(1)}, u32[]{:S(2)}, u32[]{:S(2)}) %collective-permute-start.8) | collective-permute-done | bytes 1572896 | tf_op jit(solution)/shard_map/ppermute | solution.py:35
  300.1 3.0 fusion.103
  305.7 6.8 %fusion.34 = f32[4,12,128,128]{3,2,1,0:T(8,128)S(1)} fusion(f32[4,128,12,128]{3,1,2,0:T(8,128)S(1)} %fusion.103, f32[4,12,128,128]{2,3,0,1:T(8,128)S(1)} %get-tuple-element.37), kind=kOutput, calls=%fused_computation.46 | convolution fusion | flops 1207959552 | bytes 9437184 | tf_op jit(solution)/shard_map/...ij,...jk->...ik/dot_general | solution.py:43
  312.5 6.7 %fusion.32 = f32[4,12,128,128]{3,2,1,0:T(8,128)S(1)} fusion(f32[4,128,12,128]{3,1,2,0:T(8,128)S(1)} %fusion.103, f32[4,12,128,128]{2,3,0,1:T(8,128)S(1)} %get-tuple-element.38), kind=kOutput, calls=%fused_computation.44 | convolution fusion | flops 1207959552 | bytes 9437184 | tf_op jit(solution)/shard_map/...ij,...jk->...ik/dot_general | solution.py:43
  319.2 8.6 %fusion.74 = f32[4,12,128,128]{3,2,1,0:T(8,128)} fusion(f32[4,12,128,128]{3,2,1,0:T(8,128)S(1)} %fusion.34, f32[4,12,128,128]{2,3,0,1:T(8,128)S(1)} %get-tuple-element.38, f32[4,128,12,128]{3,1,2,0:T(8,128)S(1)} %fusion.100), kind=kOutput, calls=%fused_computation.94 | convolution fusion | flops 1208745984 | bytes 12582912 | tf_op jit(solution)/shard_map/...ij,...jk->...ik/dot_general | solution.py:43
  327.8 8.4 %fusion.79 = f32[4,12,128,128]{3,2,1,0:T(8,128)} fusion(f32[4,12,128,128]{3,2,1,0:T(8,128)S(1)} %fusion.32, f32[4,12,128,128]{2,3,0,1:T(8,128)S(1)} %get-tuple-element.37, f32[4,128,12,128]{3,1,2,0:T(8,128)S(1)} %fusion.100), kind=kOutput, calls=%fused_computation.95 | convolution fusion | flops 1208745984 | bytes 12582912 | tf_op jit(solution)/shard_map/...ij,...jk->...ik/dot_general | solution.py:43
  336.1 18.5 %copy.266 = f32[4,12,128,128]{1,0,3,2:T(4,128)} copy(f32[4,12,128,128]{3,2,1,0:T(8,128)} %fusion.79) | data formatting | bytes 6291456 | tf_op jit(solution)/shard_map/add | solution.py:53
  356.8 18.5 %copy.261 = f32[4,12,128,128]{1,0,3,2:T(4,128)} copy(f32[4,12,128,128]{3,2,1,0:T(8,128)} %fusion.74) | data formatting | bytes 6291456 | tf_op jit(solution)/shard_map/sub | solution.py:52
  377.6 14.1 %psum.86 = f32[3,128]{1,0:T(4,128)S(1)} all-reduce(f32[3,128]{1,0:T(4,128)S(1)} %fusion.121), channel_id=1, replica_groups=mesh['kx'=4,'ky'=4,'kz'=2] {'ky','kz'}, use_global_device_ids=true, to_apply=%region_6.7 | all-reduce | flops 384 | bytes 3072 | tf_op jit(solution)/shard_map/psum | solution.py:120
  391.8 11.3 %psum.87 = f32[3,128]{1,0:T(4,128)S(1)} all-reduce(f32[3,128]{1,0:T(4,128)S(1)} %psum.86), channel_id=1, replica_groups=mesh['kx'=4,'ky'=4,'kz'=2] {'kx'}, use_global_device_ids=true, to_apply=%region_7.8 | all-reduce | flops 384 | bytes 3072 | tf_op jit(solution)/shard_map/psum | solution.py:119
  403.4 4.4 add_reduce_fusion.1
  416.5 18.7 %collective-permute-done.13 = f32[1,1,4,2,128,128]{5,4,2,3,1,0:T(8,128)S(1)} collective-permute-done((f32[1,1,4,2,128,128]{5,4,2,3,1,0:T(8,128)S(1)}, f32[1,1,4,2,128,128]{5,4,2,3,1,0:T(8,128)S(1)}, u32[]{:S(2)}, u32[]{:S(2)}) %collective-permute-start.13) | collective-permute-done | bytes 524320 | tf_op jit(solution)/shard_map/ppermute | solution.py:35
  438.7 3.0 fusion
  441.7 3.0 fusion.2
  444.8 3.1 fusion.109
  447.9 3.1 fusion.106
  450.9 22.6 %collective-permute-done.15 = f32[3,1,4,2,128,128]{5,4,2,3,1,0:T(8,128)S(1)} collective-permute-done((f32[3,1,4,2,128,128]{5,4,2,3,1,0:T(8,128)S(1)}, f32[3,1,4,2,128,128]{5,4,2,3,1,0:T(8,128)S(1)}, u32[]{:S(2)}, u32[]{:S(2)}) %collective-permute-start.15) | collective-permute-done | bytes 1572896 | tf_op jit(solution)/shard_map/ppermute | solution.py:33
  473.5 28.6 %collective-permute-done.14 = f32[3,1,4,2,128,128]{5,4,2,3,1,0:T(8,128)S(1)} collective-permute-done((f32[3,1,4,2,128,128]{5,4,2,3,1,0:T(8,128)S(1)}, f32[3,1,4,2,128,128]{5,4,2,3,1,0:T(8,128)S(1)}, u32[]{:S(2)}, u32[]{:S(2)}) %collective-permute-start.14) | collective-permute-done | bytes 1572896 | tf_op jit(solution)/shard_map/ppermute | solution.py:35
  508.1 3.9 fusion.26
  512.0 3.5 fusion.24
  515.5 5.3 fusion.84
  520.8 5.3 fusion.89
  526.1 18.5 %copy.294 = f32[4,12,128,128]{1,0,3,2:T(4,128)} copy(f32[4,12,128,128]{3,2,1,0:T(8,128)} %fusion.89) | data formatting | bytes 6291456 | tf_op jit(solution)/shard_map/add | solution.py:53
  546.6 18.5 %copy.289 = f32[4,12,128,128]{1,0,3,2:T(4,128)} copy(f32[4,12,128,128]{3,2,1,0:T(8,128)} %fusion.84) | data formatting | bytes 6291456 | tf_op jit(solution)/shard_map/sub | solution.py:52
  567.5 13.5 %all-reduce = (f32[3,128]{1,0:T(4,128)S(1)}, f32[128]{0:T(128)S(1)}, f32[128]{0:T(128)S(1)}, f32[128]{0:T(128)S(1)}) all-reduce(f32[3,128]{1,0:T(4,128)S(1)} %fusion.120, f32[128]{0:T(128)S(1)} %broadcast_multiply_fusion, f32[128]{0:T(128)S(1)} %broadcast_multiply_fusion.1, ...), channel_id=1, replica_groups=mesh['kx'=4,'ky'=4,'kz'=2] {'ky','kz'}, use_global_device_ids=true, to_apply=%region_11.12 | all-reduce | flops 768 | bytes 6144 | tf_op jit(solution)/shard_map/psum | solution.py:120
  581.0 12.3 %all-reduce.1 = (f32[3,128]{1,0:T(4,128)S(1)}, f32[128]{0:T(128)S(1)}, f32[128]{0:T(128)S(1)}, f32[128]{0:T(128)S(1)}) all-reduce(f32[3,128]{1,0:T(4,128)S(1)} %get-tuple-element.27, f32[128]{0:T(128)S(1)} %get-tuple-element.28, f32[128]{0:T(128)S(1)} %get-tuple-element.29, ...), channel_id=1, replica_groups=mesh['kx'=4,'ky'=4,'kz'=2] {'kx'}, use_global_device_ids=true, to_apply=%region_12.13 | all-reduce | flops 768 | bytes 6144 | tf_op jit(solution)/shard_map/psum | solution.py:119
  593.8 4.5 subtract_reduce_fusion
  (197 shorter events, 79.0 us)
Async XLA Ops:
  0.6 31.9 %copy-start.1 = (f32[1,1,4,2,128,128]{5,4,3,2,1,0:T(8,128)S(1)}, f32[1,1,4,2,128,128]{5,4,3,2,1,0:T(8,128)}, u32[]{:S(2)}) copy-start(f32[1,1,4,2,128,128]{5,4,3,2,1,0:T(8,128)} %param.3) | copy-start | bytes 1572868
  1.8 17.9 %collective-permute-start = (f32[1,1,4,2,128,128]{5,4,2,3,1,0:T(8,128)S(1)}, f32[1,1,4,2,128,128]{5,4,2,3,1,0:T(8,128)S(1)}, u32[]{:S(2)}, u32[]{:S(2)}) collective-permute-start(f32[1,1,4,2,128,128]{5,4,2,3,1,0:T(8,128)S(1)} %copy.219), channel_id=1, source_target_pairs={{0,8},{8,16},{16,24},{24,0},{1,9},{9,17},{17,25},{25,1},{2,10},{10... | collective-permute-start | bytes 1572872 | tf_op jit(solution)/shard_map/ppermute | solution.py:33
  4.9 24.6 %collective-permute-start.1 = (f32[1,1,4,2,128,128]{5,4,2,3,1,0:T(8,128)S(1)}, f32[1,1,4,2,128,128]{5,4,2,3,1,0:T(8,128)S(1)}, u32[]{:S(2)}, u32[]{:S(2)}) collective-permute-start(f32[1,1,4,2,128,128]{5,4,2,3,1,0:T(8,128)S(1)} %copy.219), channel_id=1, source_target_pairs={{8,0},{16,8},{24,16},{0,24},{9,1},{17,9},{25,17},{1,25},{10,2},{18... | collective-permute-start | bytes 1572872 | tf_op jit(solution)/shard_map/ppermute | solution.py:35
  29.6 10.1 %copy-start = (f32[1,1,4,12,2,128,128]{6,5,4,3,2,1,0:T(8,128)S(1)}, f32[1,1,4,12,2,128,128]{6,5,4,3,2,1,0:T(8,128)}, u32[]{:S(2)}) copy-start(f32[1,1,4,12,2,128,128]{6,5,4,3,2,1,0:T(8,128)} %param.4) | copy-start | bytes 18874372
  29.6 38.2 %collective-permute-start.3 = (f32[3,1,4,2,128,128]{5,4,2,3,1,0:T(8,128)S(1)}, f32[3,1,4,2,128,128]{5,4,2,3,1,0:T(8,128)S(1)}, u32[]{:S(2)}, u32[]{:S(2)}) collective-permute-start(f32[3,1,4,2,128,128]{5,4,2,3,1,0:T(8,128)S(1)} %constant_dynamic-update-slice_fusion), channel_id=1, source_target_pairs={{0,2},{2,4},{4,6},{6,0},{1,3},{3,5},{5,7},{7,1},{8,10},{10,12},{12... | collective-permute-start | bytes 4718600 | tf_op jit(solution)/shard_map/ppermute | solution.py:33
  31.1 68.9 %collective-permute-start.2 = (f32[3,1,4,2,128,128]{5,4,2,3,1,0:T(8,128)S(1)}, f32[3,1,4,2,128,128]{5,4,2,3,1,0:T(8,128)S(1)}, u32[]{:S(2)}, u32[]{:S(2)}) collective-permute-start(f32[3,1,4,2,128,128]{5,4,2,3,1,0:T(8,128)S(1)} %constant_dynamic-update-slice_fusion), channel_id=1, source_target_pairs={{2,0},{4,2},{6,4},{0,6},{3,1},{5,3},{7,5},{1,7},{10,8},{12,10},{14... | collective-permute-start | bytes 4718600 | tf_op jit(solution)/shard_map/ppermute | solution.py:35
  100.3 2.9 collective-permute-start.4
  100.4 4.5 collective-permute-start.5
  151.4 20.8 %copy-start.3 = (f32[12,3]{1,0:T(8,128)S(1)}, f32[12,3]{1,0:T(8,128)}, u32[]{:S(2)}) copy-start(f32[12,3]{1,0:T(8,128)} %constant.59.clone) | copy-start | bytes 436
  204.6 30.7 %slice-start = ((s8[6291456]{0:T(1024)(128)(4,1)}), s8[4194304]{0:T(1024)(128)(4,1)S(1)}, s32[]{:S(2)}) async-start(s8[6291456]{0:T(1024)(128)(4,1)} %bitcast.643), calls=%async_computation | async-start | bytes 8388608
  205.0 2.5 copy-start.2
  207.5 27.8 %slice-start.1 = ((s8[6291456]{0:T(1024)(128)(4,1)}), s8[2097152]{0:T(1024)(128)(4,1)S(1)}, s32[]{:S(2)}) async-start(s8[6291456]{0:T(1024)(128)(4,1)} %bitcast.643), calls=%async_computation.1 | async-start | bytes 4194304
  210.0 21.9 %collective-permute-start.7 = (f32[1,1,4,2,128,128]{4,5,2,3,1,0:T(8,128)S(1)}, f32[1,1,4,2,128,128]{4,5,2,3,1,0:T(8,128)S(1)}, u32[]{:S(2)}, u32[]{:S(2)}) collective-permute-start(f32[1,1,4,2,128,128]{4,5,2,3,1,0:T(8,128)S(1)} %pad_maximum_fusion.47), channel_id=1, source_target_pairs={{8,0},{16,8},{24,16},{0,24},{9,1},{17,9},{25,17},{1,25},{10,2},{18... | collective-permute-start | bytes 1572872 | tf_op jit(solution)/shard_map/ppermute | solution.py:35
  210.4 21.5 %collective-permute-start.6 = (f32[1,1,4,2,128,128]{4,5,2,3,1,0:T(8,128)S(1)}, f32[1,1,4,2,128,128]{4,5,2,3,1,0:T(8,128)S(1)}, u32[]{:S(2)}, u32[]{:S(2)}) collective-permute-start(f32[1,1,4,2,128,128]{4,5,2,3,1,0:T(8,128)S(1)} %pad_maximum_fusion.47), channel_id=1, source_target_pairs={{0,8},{8,16},{16,24},{24,0},{1,9},{9,17},{17,25},{25,1},{2,10},{10... | collective-permute-start | bytes 1572872 | tf_op jit(solution)/shard_map/ppermute | solution.py:33
  232.1 38.2 %collective-permute-start.9 = (f32[3,1,4,2,128,128]{4,5,2,3,1,0:T(8,128)S(1)}, f32[3,1,4,2,128,128]{4,5,2,3,1,0:T(8,128)S(1)}, u32[]{:S(2)}, u32[]{:S(2)}) collective-permute-start(f32[3,1,4,2,128,128]{4,5,2,3,1,0:T(8,128)S(1)} %pad_maximum_fusion), channel_id=1, source_target_pairs={{0,2},{2,4},{4,6},{6,0},{1,3},{3,5},{5,7},{7,1},{8,10},{10,12},{12... | collective-permute-start | bytes 4718600 | tf_op jit(solution)/shard_map/ppermute | solution.py:33
  233.6 65.7 %collective-permute-start.8 = (f32[3,1,4,2,128,128]{4,5,2,3,1,0:T(8,128)S(1)}, f32[3,1,4,2,128,128]{4,5,2,3,1,0:T(8,128)S(1)}, u32[]{:S(2)}, u32[]{:S(2)}) collective-permute-start(f32[3,1,4,2,128,128]{4,5,2,3,1,0:T(8,128)S(1)} %pad_maximum_fusion), channel_id=1, source_target_pairs={{2,0},{4,2},{6,4},{0,6},{3,1},{5,3},{7,5},{1,7},{10,8},{12,10},{14... | collective-permute-start | bytes 4718600 | tf_op jit(solution)/shard_map/ppermute | solution.py:35
  299.5 4.6 collective-permute-start.11
  299.6 4.5 collective-permute-start.10
  408.9 29.8 %slice-start.2 = ((s8[6291456]{0:T(1024)(128)(4,1)}), s8[4194304]{0:T(1024)(128)(4,1)S(1)}, s32[]{:S(2)}) async-start(s8[6291456]{0:T(1024)(128)(4,1)} %bitcast.645), calls=%async_computation.2 | async-start | bytes 8388608
  411.4 5.0 copy-start.4
  411.8 26.8 %slice-start.3 = ((s8[6291456]{0:T(1024)(128)(4,1)}), s8[2097152]{0:T(1024)(128)(4,1)S(1)}, s32[]{:S(2)}) async-start(s8[6291456]{0:T(1024)(128)(4,1)} %bitcast.645), calls=%async_computation.3 | async-start | bytes 4194304
  414.3 20.8 %collective-permute-start.13 = (f32[1,1,4,2,128,128]{5,4,2,3,1,0:T(8,128)S(1)}, f32[1,1,4,2,128,128]{5,4,2,3,1,0:T(8,128)S(1)}, u32[]{:S(2)}, u32[]{:S(2)}) collective-permute-start(f32[1,1,4,2,128,128]{5,4,2,3,1,0:T(8,128)S(1)} %pad_maximum_fusion.48), channel_id=1, source_target_pairs={{8,0},{16,8},{24,16},{0,24},{9,1},{17,9},{25,17},{1,25},{10,2},{18... | collective-permute-start | bytes 1572872 | tf_op jit(solution)/shard_map/ppermute | solution.py:35
  415.1 20.0 %collective-permute-start.12 = (f32[1,1,4,2,128,128]{5,4,2,3,1,0:T(8,128)S(1)}, f32[1,1,4,2,128,128]{5,4,2,3,1,0:T(8,128)S(1)}, u32[]{:S(2)}, u32[]{:S(2)}) collective-permute-start(f32[1,1,4,2,128,128]{5,4,2,3,1,0:T(8,128)S(1)} %pad_maximum_fusion.48), channel_id=1, source_target_pairs={{0,8},{8,16},{16,24},{24,0},{1,9},{9,17},{17,25},{25,1},{2,10},{10... | collective-permute-start | bytes 1572872 | tf_op jit(solution)/shard_map/ppermute | solution.py:33
  435.3 38.2 %collective-permute-start.15 = (f32[3,1,4,2,128,128]{5,4,2,3,1,0:T(8,128)S(1)}, f32[3,1,4,2,128,128]{5,4,2,3,1,0:T(8,128)S(1)}, u32[]{:S(2)}, u32[]{:S(2)}) collective-permute-start(f32[3,1,4,2,128,128]{5,4,2,3,1,0:T(8,128)S(1)} %pad_maximum_fusion.1), channel_id=1, source_target_pairs={{0,2},{2,4},{4,6},{6,0},{1,3},{3,5},{5,7},{7,1},{8,10},{10,12},{12... | collective-permute-start | bytes 4718600 | tf_op jit(solution)/shard_map/ppermute | solution.py:33
  436.0 66.1 %collective-permute-start.14 = (f32[3,1,4,2,128,128]{5,4,2,3,1,0:T(8,128)S(1)}, f32[3,1,4,2,128,128]{5,4,2,3,1,0:T(8,128)S(1)}, u32[]{:S(2)}, u32[]{:S(2)}) collective-permute-start(f32[3,1,4,2,128,128]{5,4,2,3,1,0:T(8,128)S(1)} %pad_maximum_fusion.1), channel_id=1, source_target_pairs={{2,0},{4,2},{6,4},{0,6},{3,1},{5,3},{7,5},{1,7},{10,8},{12,10},{14... | collective-permute-start | bytes 4718600 | tf_op jit(solution)/shard_map/ppermute | solution.py:35
  502.4 2.9 collective-permute-start.16
  502.5 4.5 collective-permute-start.17
